TPU v7x, 32 devices: a whole 2x2x4 slice. The times are simulated.
32 devices in a mesh: gx: 16 (over z, y, core), gy: 2 (over x).
Axes of the slice: x: 2, y: 2, z: 4, core: 2. Of those that a mesh axis runs over, the one named last changes fastest.
Arguments:
- right_side: float32 [16, 2, 512, 256], P('gx', 'gy'), may hold values from -8 to 8, as said below
- coords: float32 [16, 2, 2, 512], P('gx', 'gy'), may hold values from 0 to 1
- noise: float32 [16, 2, 512], P('gx', 'gy'), may hold values from 0.25 to 1
- intersect: int32 [16, 2, 128], P('gx', 'gy'), may hold values from 0 to 4607, as said below
Outputs:
- solution: float32 [16, 2, 512, 256], P('gx', 'gy')
- residual: float32 [16, 2, 512, 256], P('gx', 'gy')
Inputs may be any that keep to these rules, and one draw needn't show every extreme that they name: `right_side`: right-hand sides of order one. `intersect`: each subdomain's list holds 128 distinct indices in increasing order; none names the subdomain itself (block number 4) or a subdomain beyond the first or last one along the second dimension.
All inputs are finite; a program needn't handle non-finite values.
Results may differ from a plain program's by a relative error of at most 0.0003.
Values sent between devices are 32-bit elements; how exact they have to be, the bound alone decides.
A program may use at most 128 MiB of HBM per device.

v0:
```python
import math
import jax
import jax.numpy as jnp
from jax import lax
from jax.sharding import PartitionSpec as P

ITERS = 3
RANGE_LEN = 0.25
ROOT_THREE = math.sqrt(3.0)
HIGH = lax.Precision.HIGHEST


def shifted(value, axis, by):
    count = lax.axis_size(axis)
    return lax.ppermute(value, axis, [(i, (i + by) % count) for i in range(count)])


def passed_along(block, axis, distance):
    devices = range(lax.axis_size(axis))
    route = [(i - distance, i) for i in devices if i - distance in devices]
    return lax.ppermute(block, axis, route)


def kernel_block(rows_pos, cols_pos):
    delta_x = rows_pos[0][:, None] - cols_pos[0][None, :]
    delta_y = rows_pos[1][:, None] - cols_pos[1][None, :]
    distance = jnp.sqrt(delta_x * delta_x + delta_y * delta_y)
    scaled = ROOT_THREE / RANGE_LEN * distance
    clipped = jnp.minimum(distance, 1.0)
    taper_val = jnp.square(jnp.square(1.0 - clipped)) * (4.0 * clipped + 1.0)
    return (1.0 + scaled) * jnp.exp(-scaled) * taper_val


def window_values(values):
    beside = {}
    for step_by in (1, -1):
        beside[step_by] = shifted(values, "gx", step_by)
    column = jnp.stack([beside[1], values, beside[-1]])
    across = {}
    for step_by in (1, -1):
        across[step_by] = passed_along(column, "gy", step_by)
    return [across[1], column, across[-1]]


def window_index(values):
    beside = {}
    for step_by in (1, -1):
        beside[step_by] = shifted(values, "gx", step_by)
    column = jnp.stack([beside[1], values, beside[-1]])
    across = {}
    for step_by in (1, -1):
        across[step_by] = passed_along(column, "gy", step_by)
    return [across[1], column, across[-1]]


def column_sum(first, second):
    return jnp.sum(first * second, axis=0)


def residual_dot(residue, precond):
    return lax.psum(column_sum(residue, precond), ("gx", "gy"))


def shards(right_side, coords, noise, intersect):
    points = right_side.shape[2]
    rhs_count = right_side.shape[3]
    intersect_len = intersect.shape[2]
    ext_len = points + intersect_len
    own_pos = coords.reshape(2, points)
    own_noise = noise.reshape(points)
    point_info = jnp.concatenate([own_pos, own_noise[None, :]], axis=0)
    info_cols = window_values(point_info)
    positions = [
        [
            jnp.stack(
                [
                    info_cols[col_off][row_off, 0] + float(row_off - 1),
                    info_cols[col_off][row_off, 1] + float(col_off - 1),
                ]
            )
            for col_off in range(3)
        ]
        for row_off in range(3)
    ]
    intersect_ids = intersect.reshape(intersect_len)
    block_id = intersect_ids // points
    row_in = intersect_ids % points
    row_of = block_id // 3
    col_of = block_id % 3
    local_id = row_of * points + row_in
    picked_info = [
        jnp.take(
            jnp.transpose(info_cols[col_off], (1, 0, 2)).reshape(3, 3 * points), local_id, axis=1
        )
        for col_off in range(3)
    ]
    chosen = jnp.where(
        col_of[None, :] == 0,
        picked_info[0],
        jnp.where(col_of[None, :] == 1, picked_info[1], picked_info[2]),
    )
    ov_pos = jnp.stack(
        [chosen[0] + (row_of - 1).astype(jnp.float32), chosen[1] + (col_of - 1).astype(jnp.float32)]
    )
    ext_pos = jnp.concatenate([own_pos, ov_pos], axis=1)
    ext_noise = jnp.concatenate([own_noise, chosen[2]])
    local_matrix = kernel_block(ext_pos, ext_pos) + jnp.diag(ext_noise)
    factor = jnp.linalg.cholesky(local_matrix)
    inv_factor = lax.linalg.triangular_solve(
        factor, jnp.eye(ext_len, dtype=jnp.float32), left_side=True, lower=True
    )
    inverse = jnp.dot(inv_factor.T, inv_factor, precision=HIGH, preferred_element_type=jnp.float32)
    near_ids = window_index(intersect_ids)
    point_iota = jnp.arange(points, dtype=jnp.int32)[:, None]
    row_base = (2 - jnp.arange(3, dtype=jnp.int32))[:, None] * 3
    selectors = []
    for col_off in range(3):
        own_rows = near_ids[col_off] - (row_base + (2 - col_off)) * points
        selectors.append((point_iota == own_rows.reshape(1, 3 * intersect_len)).astype(jnp.float32))

    def borrowed_rows(residue):
        requested = [
            lax.dot_general(
                selectors[col_off],
                residue,
                (((0,), (0,)), ((), ())),
                precision=HIGH,
                preferred_element_type=jnp.float32,
            ).reshape(3, intersect_len, rhs_count)
            for col_off in range(3)
        ]
        combined = jnp.stack([requested[col_off][1] for col_off in range(3)])
        for step_by, row_off in ((-1, 0), (1, 2)):
            outgoing = jnp.stack([requested[col_off][row_off] for col_off in range(3)])
            combined = combined + shifted(outgoing, "gx", step_by)
        gathered = combined[1]
        for step_by, col_off in ((-1, 0), (1, 2)):
            gathered = gathered + passed_along(combined[col_off], "gy", step_by)
        return gathered

    def precondition(residue):
        gathered = borrowed_rows(residue)
        extended = jnp.concatenate([residue, gathered], axis=0)
        solved = jnp.dot(inverse, extended, precision=HIGH, preferred_element_type=jnp.float32)
        returned = window_values(solved[points:])
        result = solved[:points]
        for col_off in range(3):
            result = result + jnp.dot(
                selectors[col_off],
                returned[col_off].reshape(3 * intersect_len, rhs_count),
                precision=HIGH,
                preferred_element_type=jnp.float32,
            )
        return result

    noise_col = own_noise[:, None]
    residual = right_side.reshape(points, rhs_count)
    solution = jnp.zeros_like(residual)
    precond = precondition(residual)
    direction = precond
    inner_now = residual_dot(residual, precond)
    for iteration in range(ITERS):
        columns = window_values(direction)
        accumulated = noise_col * direction
        for operate_row_off in range(3):
            for operate_col_off in range(3):
                accumulated = accumulated + jnp.dot(
                    kernel_block(own_pos, positions[operate_row_off][operate_col_off]),
                    columns[operate_col_off][operate_row_off],
                    precision=HIGH,
                    preferred_element_type=jnp.float32,
                )
        step_size = inner_now / lax.psum(column_sum(direction, accumulated), ("gx", "gy"))
        solution = solution + step_size * direction
        residual = residual - step_size * accumulated
        if iteration + 1 < ITERS:
            precond = precondition(residual)
            inner_next = residual_dot(residual, precond)
            direction = precond + inner_next / inner_now * direction
            inner_now = inner_next
    return (solution.reshape(1, 1, points, rhs_count), residual.reshape(1, 1, points, rhs_count))


def solution(mesh):
    placed = (
        P("gx", "gy", None, None),
        P("gx", "gy", None, None),
        P("gx", "gy", None),
        P("gx", "gy", None),
    )
    return jax.shard_map(
        shards,
        mesh=mesh,
        in_specs=placed,
        out_specs=(P("gx", "gy", None, None), P("gx", "gy", None, None)),
        check_vma=False,
    )
```

profile of v0, /device:TPU:0, one launch (start us, length us, event | category | flops | bytes accessed | tf_op | source)
XLA Modules:
  0.0 750.6 jit_solution(9324209336027450057)
XLA Ops:
  1.2 5.0 collective-permute-start.5
  7.0 4.4 collective-permute-start.1
  15.4 4.5 collective-permute-start.6
  23.5 3.7 collective-permute-start.2
  38.7 11.7 %cholesky.132 = f32[128,128]{1,0:T(8,128)S(1)} custom-call(f32[128,128]{1,0:T(8,128)S(1)} %cholesky.337), custom_call_target="Cholesky" | custom-call | tf_op jit(solution)/shard_map/jit(cholesky)/cholesky | solution.py:108
  50.6 9.8 %custom-call.38 = f32[1,128,128]{1,2,0:T(8,128)S(1)} custom-call(f32[1,128,128]{2,1,0:T(8,128)S(1)} %get-tuple-element.83), custom_call_target="InvertDiagBlocksLowerTriangular" | custom-call | tf_op jit(solution)/shard_map/jit(cholesky)/cholesky | solution.py:108
  63.0 11.9 %cholesky.270 = f32[128,128]{1,0:T(8,128)S(1)} custom-call(f32[128,128]{1,0:T(8,128)S(1)} %cholesky.341), custom_call_target="Cholesky" | custom-call | tf_op jit(solution)/shard_map/jit(cholesky)/cholesky | solution.py:108
  76.3 9.8 %custom-call.39 = f32[1,128,128]{1,2,0:T(8,128)S(1)} custom-call(f32[1,128,128]{2,1,0:T(8,128)S(1)} %get-tuple-element.80), custom_call_target="InvertDiagBlocksLowerTriangular" | custom-call | tf_op jit(solution)/shard_map/jit(cholesky)/cholesky | solution.py:108
  87.8 11.7 %cholesky.291 = f32[128,128]{1,0:T(8,128)S(1)} custom-call(f32[128,128]{1,0:T(8,128)S(1)} %cholesky.346), custom_call_target="Cholesky" | custom-call | tf_op jit(solution)/shard_map/jit(cholesky)/cholesky | solution.py:108
  100.3 9.8 %custom-call.40 = f32[1,128,128]{1,2,0:T(8,128)S(1)} custom-call(f32[1,128,128]{2,1,0:T(8,128)S(1)} %get-tuple-element.77), custom_call_target="InvertDiagBlocksLowerTriangular" | custom-call | tf_op jit(solution)/shard_map/jit(cholesky)/cholesky | solution.py:108
  112.0 11.7 %cholesky.310 = f32[128,128]{1,0:T(8,128)S(1)} custom-call(f32[128,128]{1,0:T(8,128)S(1)} %cholesky.351), custom_call_target="Cholesky" | custom-call | tf_op jit(solution)/shard_map/jit(cholesky)/cholesky | solution.py:108
  124.4 9.8 %custom-call.41 = f32[1,128,128]{1,2,0:T(8,128)S(1)} custom-call(f32[1,128,128]{2,1,0:T(8,128)S(1)} %get-tuple-element.74), custom_call_target="InvertDiagBlocksLowerTriangular" | custom-call | tf_op jit(solution)/shard_map/jit(cholesky)/cholesky | solution.py:108
  135.7 11.7 %cholesky.327 = f32[128,128]{1,0:T(8,128)S(1)} custom-call(f32[128,128]{1,0:T(8,128)S(1)} %convolution_subtract_fusion.6), custom_call_target="Cholesky" | custom-call | tf_op jit(solution)/shard_map/jit(cholesky)/cholesky | solution.py:108
  152.5 17.8 %while.1 = (s32[]{:T(128)}, f32[640,640]{1,0:T(8,128)}, s32[5,2]{0,1:T(2,128)S(1)}, f32[5,128,128]{2,1,0:T(8,128)}, s32[]{:T(128)}) while((s32[]{:T(128)}, f32[640,640]{1,0:T(8,128)}, s32[5,2]{0,1:T(2,128)S(1)}, f32[5,128,128]{2,1,0:T(8,128)}, s32[]{:T(128)}) %tuple.96), condition=%wide.while_cond, body=%wide.while_body.sunk | while | flops 2 | bytes 132705 | solution.py:109
  170.3 50.7 %custom-call.42 = f32[5,128,128]{1,2,0:T(8,128)} custom-call(f32[5,128,128]{2,1,0:T(8,128)} %get-tuple-element.10), custom_call_target="InvertDiagBlocksLowerTriangular" | custom-call | tf_op jit(solution)/shard_map/triangular_solve | solution.py:109
  234.1 4.7 collective-permute-start.11
  238.8 5.0 fusion.240
  245.7 4.4 collective-permute-start.13
  260.4 3.8 collective-permute-done.15
  264.9 4.4 collective-permute-start.17
  269.3 6.9 collective-permute-done.16
  285.3 26.6 %collective-permute-done.18 = f32[3,512,256]{2,1,0:T(8,128)S(1)} collective-permute-done((f32[3,512,256]{2,1,0:T(8,128)S(1)}, f32[3,512,256]{2,1,0:T(8,128)S(1)}, u32[]{:S(2)}, u32[]{:S(2)}) %collective-permute-start.18) | collective-permute-done | bytes 1572896 | tf_op jit(solution)/shard_map/ppermute | solution.py:21
  324.3 40.9 %all-reduce.1 = (f32[256]{0:T(256)S(1)}, f32[256]{0:T(256)S(1)}) all-reduce(f32[256]{0:T(256)S(1)} %get-tuple-element.12, f32[256]{0:T(256)S(1)} %get-tuple-element.11), channel_id=1, replica_groups=mesh['gx'=16,'gy'=2] {'gx','gy'}, use_global_device_ids=true, to_apply=%region_11.13 | all-reduce | flops 512 | bytes 4096 | tf_op jit(solution)/shard_map/psum | solution.py:61
  369.6 5.2 collective-permute-done.20
  374.7 4.8 collective-permute-done.21
  380.9 4.6 collective-permute-start.23
  391.3 4.1 collective-permute-start.25
  398.2 4.4 collective-permute-start.26
  404.5 7.1 collective-permute-done.26
  412.3 3.5 collective-permute-done.27
  417.2 36.8 %psum.44 = f32[256]{0:T(256)S(1)} all-reduce(f32[256]{0:T(256)S(1)} %get-tuple-element.128), channel_id=1, replica_groups=mesh['gx'=16,'gy'=2] {'gx','gy'}, use_global_device_ids=true, to_apply=%region_15.17 | all-reduce | flops 256 | bytes 2048 | tf_op jit(solution)/shard_map/psum | solution.py:61
  455.2 4.4 collective-permute-start.29
  459.6 7.0 collective-permute-done.28
  466.7 4.3 collective-permute-start.30
  478.3 24.6 %collective-permute-done.30 = f32[3,512,256]{2,1,0:T(8,128)S(1)} collective-permute-done((f32[3,512,256]{2,1,0:T(8,128)S(1)}, f32[3,512,256]{2,1,0:T(8,128)S(1)}, u32[]{:S(2)}, u32[]{:S(2)}) %collective-permute-start.30) | collective-permute-done | bytes 1572896 | tf_op jit(solution)/shard_map/ppermute | solution.py:21
  515.2 43.2 %psum.45 = f32[256]{0:T(256)S(1)} all-reduce(f32[256]{0:T(256)S(1)} %get-tuple-element.130), channel_id=1, replica_groups=mesh['gx'=16,'gy'=2] {'gx','gy'}, use_global_device_ids=true, to_apply=%region_17.19 | all-reduce | flops 256 | bytes 2048 | tf_op jit(solution)/shard_map/psum | solution.py:173
  562.8 5.2 collective-permute-done.32
  568.0 4.8 collective-permute-done.33
  574.2 4.6 collective-permute-start.35
  584.5 4.1 collective-permute-start.37
  591.4 4.4 collective-permute-start.38
  597.8 6.8 collective-permute-done.38
  609.4 36.9 %psum.46 = f32[256]{0:T(256)S(1)} all-reduce(f32[256]{0:T(256)S(1)} %get-tuple-element.132), channel_id=1, replica_groups=mesh['gx'=16,'gy'=2] {'gx','gy'}, use_global_device_ids=true, to_apply=%region_19.21 | all-reduce | flops 256 | bytes 2048 | tf_op jit(solution)/shard_map/psum | solution.py:61
  646.4 4.4 collective-permute-start.41
  650.8 7.0 collective-permute-done.40
  657.9 4.3 collective-permute-start.42
  669.3 25.0 %collective-permute-done.42 = f32[3,512,256]{2,1,0:T(8,128)S(1)} collective-permute-done((f32[3,512,256]{2,1,0:T(8,128)S(1)}, f32[3,512,256]{2,1,0:T(8,128)S(1)}, u32[]{:S(2)}, u32[]{:S(2)}) %collective-permute-start.42) | collective-permute-done | bytes 1572896 | tf_op jit(solution)/shard_map/ppermute | solution.py:21
  705.9 43.1 %psum.47 = f32[256]{0:T(256)S(1)} all-reduce(f32[256]{0:T(256)S(1)} %get-tuple-element.134), channel_id=1, replica_groups=mesh['gx'=16,'gy'=2] {'gx','gy'}, use_global_device_ids=true, to_apply=%region_21.23 | all-reduce | flops 256 | bytes 2048 | tf_op jit(solution)/shard_map/psum | solution.py:173
  (255 shorter events, 177.0 us)
Async XLA Ops:
  0.6 19.3 %copy-start = (f32[1,1,512,256]{3,2,1,0:T(8,128)S(1)}, f32[1,1,512,256]{3,2,1,0:T(8,128)}, u32[]{:S(2)}) copy-start(f32[1,1,512,256]{3,2,1,0:T(8,128)} %param.6) | copy-start | bytes 1572868
  0.7 13.4 %collective-permute-start.4 = (s32[128]{0:T(128)}, s32[128]{0:T(128)S(1)}, u32[]{:S(2)}, u32[]{:S(2)}) collective-permute-start(s32[128]{0:T(128)} %bitcast.373), channel_id=1, source_target_pairs={{0,2},{2,4},{4,6},{6,8},{8,10},{10,12},{12,14},{14,16},{16,18},{18... | collective-permute-start | bytes 1544 | tf_op jit(solution)/shard_map/ppermute | solution.py:15
  1.2 12.8 %collective-permute-start.5 = (s32[128]{0:T(128)}, s32[128]{0:T(128)S(1)}, u32[]{:S(2)}, u32[]{:S(2)}) collective-permute-start(s32[128]{0:T(128)} %bitcast.374), channel_id=1, source_target_pairs={{0,30},{2,0},{4,2},{6,4},{8,6},{10,8},{12,10},{14,12},{16,14},{18,... | collective-permute-start | bytes 1544 | tf_op jit(solution)/shard_map/ppermute | solution.py:15
  7.0 16.5 %collective-permute-start = (f32[3,512]{1,0:T(4,128)S(1)}, f32[3,512]{1,0:T(4,128)S(1)}, u32[]{:S(2)}, u32[]{:S(2)}) collective-permute-start(f32[3,512]{1,0:T(4,128)S(1)} %get-tuple-element.110), channel_id=1, source_target_pairs={{0,2},{2,4},{4,6},{6,8},{8,10},{10,12},{12,14},{14,16},{16,18},{18... | collective-permute-start | bytes 18440 | tf_op jit(solution)/shard_map/ppermute | solution.py:15
  7.0 16.4 %collective-permute-start.1 = (f32[3,512]{1,0:T(4,128)S(1)}, f32[3,512]{1,0:T(4,128)S(1)}, u32[]{:S(2)}, u32[]{:S(2)}) collective-permute-start(f32[3,512]{1,0:T(4,128)S(1)} %get-tuple-element.110), channel_id=1, source_target_pairs={{0,30},{2,0},{4,2},{6,4},{8,6},{10,8},{12,10},{14,12},{16,14},{18,... | collective-permute-start | bytes 18440 | tf_op jit(solution)/shard_map/ppermute | solution.py:15
  14.1 6.7 collective-permute-start.7
  15.4 6.3 collective-permute-start.6
  23.5 208.1 %collective-permute-start.8 = (f32[3,128,256]{2,1,0:T(8,128)}, f32[3,128,256]{2,1,0:T(8,128)}, u32[]{:S(2)}, u32[]{:S(2)}) collective-permute-start(f32[3,128,256]{2,1,0:T(8,128)} %pad_maximum_fusion.3), channel_id=1, source_target_pairs={{0,30},{2,0},{4,2},{6,4},{8,6},{10,8},{12,10},{14,12},{16,14},{18,... | collective-permute-start | bytes 1179656 | tf_op jit(solution)/shard_map/ppermute | solution.py:15
  23.5 7.5 collective-permute-start.2
  27.2 5.7 collective-permute-start.3
  29.3 202.3 %collective-permute-start.9 = (f32[3,128,256]{2,1,0:T(8,128)}, f32[3,128,256]{2,1,0:T(8,128)}, u32[]{:S(2)}, u32[]{:S(2)}) collective-permute-start(f32[3,128,256]{2,1,0:T(8,128)} %pad_maximum_fusion.4), channel_id=1, source_target_pairs={{0,2},{2,4},{4,6},{6,8},{8,10},{10,12},{12,14},{14,16},{16,18},{18... | collective-permute-start | bytes 1179656 | tf_op jit(solution)/shard_map/ppermute | solution.py:15
  170.3 54.7 %copy-start.3 = (f32[640,640]{1,0:T(8,128)S(1)}, f32[640,640]{1,0:T(8,128)}, u32[]{:S(2)}) copy-start(f32[640,640]{1,0:T(8,128)} %fusion.25) | copy-start | bytes 4915204
  232.8 11.1 %collective-permute-start.10 = (f32[128,256]{1,0:T(8,128)S(1)}, f32[128,256]{1,0:T(8,128)S(1)}, u32[]{:S(2)}, u32[]{:S(2)}) collective-permute-start(f32[128,256]{1,0:T(8,128)S(1)} %get-tuple-element.60), channel_id=1, source_target_pairs={{1,0},{3,2},{5,4},{7,6},{9,8},{11,10},{13,12},{15,14},{17,16},{19,... | collective-permute-start | bytes 393224 | tf_op jit(solution)/shard_map/ppermute | solution.py:21
  234.1 9.8 %collective-permute-start.11 = (f32[128,256]{1,0:T(8,128)S(1)}, f32[128,256]{1,0:T(8,128)S(1)}, u32[]{:S(2)}, u32[]{:S(2)}) collective-permute-start(f32[128,256]{1,0:T(8,128)S(1)} %get-tuple-element.61), channel_id=1, source_target_pairs={{0,1},{2,3},{4,5},{6,7},{8,9},{10,11},{12,13},{14,15},{16,17},{18,... | collective-permute-start | bytes 393224 | tf_op jit(solution)/shard_map/ppermute | solution.py:21
  245.7 7.1 collective-permute-start.12
  245.7 7.1 collective-permute-start.13
  252.9 6.9 collective-permute-start.14
  254.5 9.7 %collective-permute-start.15 = (f32[3,128,256]{2,1,0:T(8,128)S(1)}, f32[3,128,256]{2,1,0:T(8,128)S(1)}, u32[]{:S(2)}, u32[]{:S(2)}) collective-permute-start(f32[3,128,256]{2,1,0:T(8,128)S(1)} %pad_maximum_fusion.5), channel_id=1, source_target_pairs={{1,0},{3,2},{5,4},{7,6},{9,8},{11,10},{13,12},{15,14},{17,16},{19,... | collective-permute-start | bytes 1179656 | tf_op jit(solution)/shard_map/ppermute | solution.py:21
  264.8 11.5 %collective-permute-start.16 = (f32[512,256]{1,0:T(8,128)S(1)}, f32[512,256]{1,0:T(8,128)S(1)}, u32[]{:S(2)}, u32[]{:S(2)}) collective-permute-start(f32[512,256]{1,0:T(8,128)S(1)} %convolution_add_fusion.5), channel_id=1, source_target_pairs={{0,2},{2,4},{4,6},{6,8},{8,10},{10,12},{12,14},{14,16},{16,18},{18... | collective-permute-start | bytes 1572872 | tf_op jit(solution)/shard_map/ppermute | solution.py:15
  264.9 11.4 %collective-permute-start.17 = (f32[512,256]{1,0:T(8,128)S(1)}, f32[512,256]{1,0:T(8,128)S(1)}, u32[]{:S(2)}, u32[]{:S(2)}) collective-permute-start(f32[512,256]{1,0:T(8,128)S(1)} %convolution_add_fusion.5), channel_id=1, source_target_pairs={{0,30},{2,0},{4,2},{6,4},{8,6},{10,8},{12,10},{14,12},{16,14},{18,... | collective-permute-start | bytes 1572872 | tf_op jit(solution)/shard_map/ppermute | solution.py:15
  276.4 35.5 %collective-permute-start.18 = (f32[3,512,256]{2,1,0:T(8,128)S(1)}, f32[3,512,256]{2,1,0:T(8,128)S(1)}, u32[]{:S(2)}, u32[]{:S(2)}) collective-permute-start(f32[3,512,256]{2,1,0:T(8,128)S(1)} %pad_maximum_fusion), channel_id=1, source_target_pairs={{0,1},{2,3},{4,5},{6,7},{8,9},{10,11},{12,13},{14,15},{16,17},{18,... | collective-permute-start | bytes 4718600 | tf_op jit(solution)/shard_map/ppermute | solution.py:21
  278.0 39.5 %collective-permute-start.19 = (f32[3,512,256]{2,1,0:T(8,128)S(1)}, f32[3,512,256]{2,1,0:T(8,128)S(1)}, u32[]{:S(2)}, u32[]{:S(2)}) collective-permute-start(f32[3,512,256]{2,1,0:T(8,128)S(1)} %pad_maximum_fusion), channel_id=1, source_target_pairs={{1,0},{3,2},{5,4},{7,6},{9,8},{11,10},{13,12},{15,14},{17,16},{19,... | collective-permute-start | bytes 4718600 | tf_op jit(solution)/shard_map/ppermute | solution.py:21
  368.9 5.8 collective-permute-start.20
  369.5 10.1 %collective-permute-start.21 = (f32[3,128,256]{2,1,0:T(8,128)S(1)}, f32[3,128,256]{2,1,0:T(8,128)S(1)}, u32[]{:S(2)}, u32[]{:S(2)}) collective-permute-start(f32[3,128,256]{2,1,0:T(8,128)S(1)} %pad_maximum_fusion.7), channel_id=1, source_target_pairs={{0,2},{2,4},{4,6},{6,8},{8,10},{10,12},{12,14},{14,16},{16,18},{18... | collective-permute-start | bytes 1179656 | tf_op jit(solution)/shard_map/ppermute | solution.py:15
  379.6 7.7 %collective-permute-start.22 = (f32[128,256]{1,0:T(8,128)S(1)}, f32[128,256]{1,0:T(8,128)S(1)}, u32[]{:S(2)}, u32[]{:S(2)}) collective-permute-start(f32[128,256]{1,0:T(8,128)S(1)} %get-tuple-element.49), channel_id=1, source_target_pairs={{1,0},{3,2},{5,4},{7,6},{9,8},{11,10},{13,12},{15,14},{17,16},{19,... | collective-permute-start | bytes 393224 | tf_op jit(solution)/shard_map/ppermute | solution.py:21
  380.9 8.2 %collective-permute-start.23 = (f32[128,256]{1,0:T(8,128)S(1)}, f32[128,256]{1,0:T(8,128)S(1)}, u32[]{:S(2)}, u32[]{:S(2)}) collective-permute-start(f32[128,256]{1,0:T(8,128)S(1)} %get-tuple-element.50), channel_id=1, source_target_pairs={{0,1},{2,3},{4,5},{6,7},{8,9},{10,11},{12,13},{14,15},{16,17},{18,... | collective-permute-start | bytes 393224 | tf_op jit(solution)/shard_map/ppermute | solution.py:21
  390.9 7.2 collective-permute-start.24
  391.3 6.8 collective-permute-start.25
  398.2 13.5 %collective-permute-start.26 = (f32[3,128,256]{2,1,0:T(8,128)S(1)}, f32[3,128,256]{2,1,0:T(8,128)S(1)}, u32[]{:S(2)}, u32[]{:S(2)}) collective-permute-start(f32[3,128,256]{2,1,0:T(8,128)S(1)} %pad_maximum_fusion.8), channel_id=1, source_target_pairs={{0,1},{2,3},{4,5},{6,7},{8,9},{10,11},{12,13},{14,15},{16,17},{18,... | collective-permute-start | bytes 1179656 | tf_op jit(solution)/shard_map/ppermute | solution.py:21
  402.6 13.2 %collective-permute-start.27 = (f32[3,128,256]{2,1,0:T(8,128)S(1)}, f32[3,128,256]{2,1,0:T(8,128)S(1)}, u32[]{:S(2)}, u32[]{:S(2)}) collective-permute-start(f32[3,128,256]{2,1,0:T(8,128)S(1)} %pad_maximum_fusion.8), channel_id=1, source_target_pairs={{1,0},{3,2},{5,4},{7,6},{9,8},{11,10},{13,12},{15,14},{17,16},{19,... | collective-permute-start | bytes 1179656 | tf_op jit(solution)/shard_map/ppermute | solution.py:21
  455.1 57.2 %copy-start.1 = (f32[512,256]{1,0:T(8,128)}, f32[512,256]{1,0:T(8,128)S(1)}, u32[]{:S(2)}) copy-start(f32[512,256]{1,0:T(8,128)S(1)} %multiply_add_fusion.1) | copy-start | bytes 1572868
  455.1 11.5 %collective-permute-start.28 = (f32[512,256]{1,0:T(8,128)S(1)}, f32[512,256]{1,0:T(8,128)S(1)}, u32[]{:S(2)}, u32[]{:S(2)}) collective-permute-start(f32[512,256]{1,0:T(8,128)S(1)} %multiply_add_fusion.1), channel_id=1, source_target_pairs={{0,2},{2,4},{4,6},{6,8},{8,10},{10,12},{12,14},{14,16},{16,18},{18... | collective-permute-start | bytes 1572872 | tf_op jit(solution)/shard_map/ppermute | solution.py:15
  455.2 11.4 %collective-permute-start.29 = (f32[512,256]{1,0:T(8,128)S(1)}, f32[512,256]{1,0:T(8,128)S(1)}, u32[]{:S(2)}, u32[]{:S(2)}) collective-permute-start(f32[512,256]{1,0:T(8,128)S(1)} %multiply_add_fusion.1), channel_id=1, source_target_pairs={{0,30},{2,0},{4,2},{6,4},{8,6},{10,8},{12,10},{14,12},{16,14},{18,... | collective-permute-start | bytes 1572872 | tf_op jit(solution)/shard_map/ppermute | solution.py:15
  466.7 36.1 %collective-permute-start.30 = (f32[3,512,256]{2,1,0:T(8,128)S(1)}, f32[3,512,256]{2,1,0:T(8,128)S(1)}, u32[]{:S(2)}, u32[]{:S(2)}) collective-permute-start(f32[3,512,256]{2,1,0:T(8,128)S(1)} %pad_maximum_fusion.1), channel_id=1, source_target_pairs={{0,1},{2,3},{4,5},{6,7},{8,9},{10,11},{12,13},{14,15},{16,17},{18,... | collective-permute-start | bytes 4718600 | tf_op jit(solution)/shard_map/ppermute | solution.py:21
  471.0 37.4 %collective-permute-start.31 = (f32[3,512,256]{2,1,0:T(8,128)S(1)}, f32[3,512,256]{2,1,0:T(8,128)S(1)}, u32[]{:S(2)}, u32[]{:S(2)}) collective-permute-start(f32[3,512,256]{2,1,0:T(8,128)S(1)} %pad_maximum_fusion.1), channel_id=1, source_target_pairs={{1,0},{3,2},{5,4},{7,6},{9,8},{11,10},{13,12},{15,14},{17,16},{19,... | collective-permute-start | bytes 4718600 | tf_op jit(solution)/shard_map/ppermute | solution.py:21
  562.1 5.9 collective-permute-start.32
  562.7 10.1 %collective-permute-start.33 = (f32[3,128,256]{2,1,0:T(8,128)S(1)}, f32[3,128,256]{2,1,0:T(8,128)S(1)}, u32[]{:S(2)}, u32[]{:S(2)}) collective-permute-start(f32[3,128,256]{2,1,0:T(8,128)S(1)} %pad_maximum_fusion.10), channel_id=1, source_target_pairs={{0,2},{2,4},{4,6},{6,8},{8,10},{10,12},{12,14},{14,16},{16,18},{18... | collective-permute-start | bytes 1179656 | tf_op jit(solution)/shard_map/ppermute | solution.py:15
  572.9 7.8 %collective-permute-start.34 = (f32[128,256]{1,0:T(8,128)S(1)}, f32[128,256]{1,0:T(8,128)S(1)}, u32[]{:S(2)}, u32[]{:S(2)}) collective-permute-start(f32[128,256]{1,0:T(8,128)S(1)} %get-tuple-element.38), channel_id=1, source_target_pairs={{1,0},{3,2},{5,4},{7,6},{9,8},{11,10},{13,12},{15,14},{17,16},{19,... | collective-permute-start | bytes 393224 | tf_op jit(solution)/shard_map/ppermute | solution.py:21
  574.2 8.2 %collective-permute-start.35 = (f32[128,256]{1,0:T(8,128)S(1)}, f32[128,256]{1,0:T(8,128)S(1)}, u32[]{:S(2)}, u32[]{:S(2)}) collective-permute-start(f32[128,256]{1,0:T(8,128)S(1)} %get-tuple-element.39), channel_id=1, source_target_pairs={{0,1},{2,3},{4,5},{6,7},{8,9},{10,11},{12,13},{14,15},{16,17},{18,... | collective-permute-start | bytes 393224 | tf_op jit(solution)/shard_map/ppermute | solution.py:21
  584.2 7.2 collective-permute-start.36
  584.5 6.9 collective-permute-start.37
  591.4 13.1 %collective-permute-start.38 = (f32[3,128,256]{2,1,0:T(8,128)S(1)}, f32[3,128,256]{2,1,0:T(8,128)S(1)}, u32[]{:S(2)}, u32[]{:S(2)}) collective-permute-start(f32[3,128,256]{2,1,0:T(8,128)S(1)} %pad_maximum_fusion.11), channel_id=1, source_target_pairs={{0,1},{2,3},{4,5},{6,7},{8,9},{10,11},{12,13},{14,15},{16,17},{18,... | collective-permute-start | bytes 1179656 | tf_op jit(solution)/shard_map/ppermute | solution.py:21
  595.9 12.8 %collective-permute-start.39 = (f32[3,128,256]{2,1,0:T(8,128)S(1)}, f32[3,128,256]{2,1,0:T(8,128)S(1)}, u32[]{:S(2)}, u32[]{:S(2)}) collective-permute-start(f32[3,128,256]{2,1,0:T(8,128)S(1)} %pad_maximum_fusion.11), channel_id=1, source_target_pairs={{1,0},{3,2},{5,4},{7,6},{9,8},{11,10},{13,12},{15,14},{17,16},{19,... | collective-permute-start | bytes 1179656 | tf_op jit(solution)/shard_map/ppermute | solution.py:21
  605.2 41.1 %copy-start.2 = (f32[512,256]{1,0:T(8,128)S(1)}, f32[512,256]{1,0:T(8,128)}, u32[]{:S(2)}) copy-start(f32[512,256]{1,0:T(8,128)} %copy-done.1) | copy-start | bytes 1572868
  646.3 11.5 %collective-permute-start.40 = (f32[512,256]{1,0:T(8,128)S(1)}, f32[512,256]{1,0:T(8,128)S(1)}, u32[]{:S(2)}, u32[]{:S(2)}) collective-permute-start(f32[512,256]{1,0:T(8,128)S(1)} %multiply_add_fusion), channel_id=1, source_target_pairs={{0,2},{2,4},{4,6},{6,8},{8,10},{10,12},{12,14},{14,16},{16,18},{18... | collective-permute-start | bytes 1572872 | tf_op jit(solution)/shard_map/ppermute | solution.py:15
  646.4 11.4 %collective-permute-start.41 = (f32[512,256]{1,0:T(8,128)S(1)}, f32[512,256]{1,0:T(8,128)S(1)}, u32[]{:S(2)}, u32[]{:S(2)}) collective-permute-start(f32[512,256]{1,0:T(8,128)S(1)} %multiply_add_fusion), channel_id=1, source_target_pairs={{0,30},{2,0},{4,2},{6,4},{8,6},{10,8},{12,10},{14,12},{16,14},{18,... | collective-permute-start | bytes 1572872 | tf_op jit(solution)/shard_map/ppermute | solution.py:15
  657.9 36.3 %collective-permute-start.42 = (f32[3,512,256]{2,1,0:T(8,128)S(1)}, f32[3,512,256]{2,1,0:T(8,128)S(1)}, u32[]{:S(2)}, u32[]{:S(2)}) collective-permute-start(f32[3,512,256]{2,1,0:T(8,128)S(1)} %pad_maximum_fusion.2), channel_id=1, source_target_pairs={{0,1},{2,3},{4,5},{6,7},{8,9},{10,11},{12,13},{14,15},{16,17},{18,... | collective-permute-start | bytes 4718600 | tf_op jit(solution)/shard_map/ppermute | solution.py:21
  662.2 37.6 %collective-permute-start.43 = (f32[3,512,256]{2,1,0:T(8,128)S(1)}, f32[3,512,256]{2,1,0:T(8,128)S(1)}, u32[]{:S(2)}, u32[]{:S(2)}) collective-permute-start(f32[3,512,256]{2,1,0:T(8,128)S(1)} %pad_maximum_fusion.2), channel_id=1, source_target_pairs={{1,0},{3,2},{5,4},{7,6},{9,8},{11,10},{13,12},{15,14},{17,16},{19,... | collective-permute-start | bytes 4718600 | tf_op jit(solution)/shard_map/ppermute | solution.py:21
  (5 other events, 28.6 us)
where the time goes:
time: 756 us; the launch traced here: 751 us
  blocking collectives  201 us (27%)
  other arithmetic  168 us (22%)
  waiting for transfers between devices  161 us (21%)
  starting transfers between devices  96.9 us (13%)
  matrix products  94.8 us (13%)
  local copies, waits for them, and re-layouts  22.5 us (3%)
    psum x3, blocking collectives, residual_dot(): return lax.psum(column_sum(residue, precond), ('gx', 'gy'))  115 us
    ppermute x22, waiting for transfers between devices, passed_along(): return lax.ppermute(block, axis, route)  112 us
    another operation x19, other arithmetic, shards(): factor = jnp.linalg.cholesky(local_matrix)  101 us
    psum x2, blocking collectives, shards(): lax.psum(column_sum(direction, accumulated), ('gx', 'gy'))  86.3 us
    ppermute x22, starting transfers between devices, passed_along(): return lax.ppermute(block, axis, route)  57.9 us
    dot_general x27, matrix products, shards(): jnp.dot(kernel_block(own_pos, positions[operate_row_off][operate_col_off]...  52.9 us
    another operation x3, other arithmetic, shards(): lax.linalg.triangular_solve(factor, jnp.eye(ext_len, dtype=jnp.float32),...  52 us
    ppermute x22, waiting for transfers between devices, shifted(): lax.ppermute(value, axis, [(i, (i + by) % count) for i in range(count)])  49 us
  transfers between devices with their start and end apart: 44, of which 24 were waited for; matrix products, arithmetic and copies ran while one was open for 33% of the time, Pallas kernels for 0%

commit v1 on v0

--- a/solution.py
+++ b/solution.py
@@ -170,7 +170,15 @@
                     precision=HIGH,
                     preferred_element_type=jnp.float32,
                 )
-        step_size = inner_now / lax.psum(column_sum(direction, accumulated), ("gx", "gy"))
+
+        def manage_chains(my_data):
+            axis_name = "gy"
+            shard_axis = "gx"
+            for c in (shard_axis, axis_name):
+                my_data = jax.lax.psum(my_data, axis_name=c)
+            return my_data
+
+        step_size = inner_now / manage_chains(column_sum(direction, accumulated))
         solution = solution + step_size * direction
         residual = residual - step_size * accumulated
         if iteration + 1 < ITERS:

time: 756 us -> 780 us (1.032)
  blocking collectives: 201 us -> 232 us
  waiting for transfers between devices: 161 us -> 152 us
    psum x2 -> x6, blocking collectives: 86.3 us -> 119 us  [manage_chains(): my_data = jax.lax.psum(my_data, axis_name=c)]
    ppermute x22, waiting for transfers between devices: 112 us -> 104 us  [passed_along(): return lax.ppermute(block, axis, route)]
  transfers between devices with their start and end apart: 44 -> 44, of which waited for: 24 -> 24; matrix products, arithmetic and copies ran while one was open for 33% -> 32% of each run, Pallas kernels for 0% -> 0%
where the time goes in v1:
time: 780 us; the launch traced here: 775 us
  blocking collectives  232 us (30%)
  other arithmetic  168 us (22%)
  waiting for transfers between devices  152 us (19%)
  starting transfers between devices  99.4 us (13%)
  matrix products  94.8 us (12%)
  local copies, waits for them, and re-layouts  22.7 us (3%)
    psum x6, blocking collectives, manage_chains(): my_data = jax.lax.psum(my_data, axis_name=c)  119 us
    psum x3, blocking collectives, residual_dot(): return lax.psum(column_sum(residue, precond), ('gx', 'gy'))  114 us
    ppermute x22, waiting for transfers between devices, passed_along(): return lax.ppermute(block, axis, route)  104 us
    another operation x19, other arithmetic, shards(): factor = jnp.linalg.cholesky(local_matrix)  101 us
    ppermute x22, starting transfers between devices, passed_along(): return lax.ppermute(block, axis, route)  57.8 us
    dot_general x27, matrix products, shards(): jnp.dot(kernel_block(own_pos, positions[operate_row_off][operate_col_off]...  52.9 us
    another operation x3, other arithmetic, shards(): lax.linalg.triangular_solve(factor, jnp.eye(ext_len, dtype=jnp.float32),...  52 us
    ppermute x22, waiting for transfers between devices, shifted(): lax.ppermute(value, axis, [(i, (i + by) % count) for i in range(count)])  48.1 us
  transfers between devices with their start and end apart: 44, of which 24 were waited for; matrix products, arithmetic and copies ran while one was open for 32% of the time, Pallas kernels for 0%

profile of v1, /device:TPU:0, one launch (start us, length us, event | category | flops | bytes accessed | tf_op | source)
XLA Modules:
  0.0 775.2 jit_solution(3295732440265664145)
XLA Ops:
  1.2 5.0 collective-permute-start.5
  7.0 4.4 collective-permute-start.1
  15.4 4.5 collective-permute-start.6
  38.7 11.7 %cholesky.132 = f32[128,128]{1,0:T(8,128)S(1)} custom-call(f32[128,128]{1,0:T(8,128)S(1)} %cholesky.337), custom_call_target="Cholesky" | custom-call | tf_op jit(solution)/shard_map/jit(cholesky)/cholesky | solution.py:108
  50.5 9.8 %custom-call.38 = f32[1,128,128]{1,2,0:T(8,128)S(1)} custom-call(f32[1,128,128]{2,1,0:T(8,128)S(1)} %get-tuple-element.81), custom_call_target="InvertDiagBlocksLowerTriangular" | custom-call | tf_op jit(solution)/shard_map/jit(cholesky)/cholesky | solution.py:108
  63.0 11.9 %cholesky.270 = f32[128,128]{1,0:T(8,128)S(1)} custom-call(f32[128,128]{1,0:T(8,128)S(1)} %cholesky.341), custom_call_target="Cholesky" | custom-call | tf_op jit(solution)/shard_map/jit(cholesky)/cholesky | solution.py:108
  76.3 9.8 %custom-call.39 = f32[1,128,128]{1,2,0:T(8,128)S(1)} custom-call(f32[1,128,128]{2,1,0:T(8,128)S(1)} %get-tuple-element.78), custom_call_target="InvertDiagBlocksLowerTriangular" | custom-call | tf_op jit(solution)/shard_map/jit(cholesky)/cholesky | solution.py:108
  87.8 11.7 %cholesky.291 = f32[128,128]{1,0:T(8,128)S(1)} custom-call(f32[128,128]{1,0:T(8,128)S(1)} %cholesky.346), custom_call_target="Cholesky" | custom-call | tf_op jit(solution)/shard_map/jit(cholesky)/cholesky | solution.py:108
  100.2 9.8 %custom-call.40 = f32[1,128,128]{1,2,0:T(8,128)S(1)} custom-call(f32[1,128,128]{2,1,0:T(8,128)S(1)} %get-tuple-element.75), custom_call_target="InvertDiagBlocksLowerTriangular" | custom-call | tf_op jit(solution)/shard_map/jit(cholesky)/cholesky | solution.py:108
  111.9 11.7 %cholesky.310 = f32[128,128]{1,0:T(8,128)S(1)} custom-call(f32[128,128]{1,0:T(8,128)S(1)} %cholesky.351), custom_call_target="Cholesky" | custom-call | tf_op jit(solution)/shard_map/jit(cholesky)/cholesky | solution.py:108
  124.3 9.8 %custom-call.41 = f32[1,128,128]{1,2,0:T(8,128)S(1)} custom-call(f32[1,128,128]{2,1,0:T(8,128)S(1)} %get-tuple-element.72), custom_call_target="InvertDiagBlocksLowerTriangular" | custom-call | tf_op jit(solution)/shard_map/jit(cholesky)/cholesky | solution.py:108
  135.6 11.7 %cholesky.327 = f32[128,128]{1,0:T(8,128)S(1)} custom-call(f32[128,128]{1,0:T(8,128)S(1)} %convolution_subtract_fusion.6), custom_call_target="Cholesky" | custom-call | tf_op jit(solution)/shard_map/jit(cholesky)/cholesky | solution.py:108
  152.2 18.0 %while.1 = (s32[]{:T(128)}, f32[640,640]{1,0:T(8,128)}, s32[5,2]{0,1:T(2,128)S(1)}, f32[5,128,128]{2,1,0:T(8,128)}, s32[]{:T(128)}) while((s32[]{:T(128)}, f32[640,640]{1,0:T(8,128)}, s32[5,2]{0,1:T(2,128)S(1)}, f32[5,128,128]{2,1,0:T(8,128)}, s32[]{:T(128)}) %tuple.96), condition=%wide.while_cond, body=%wide.while_body.sunk | while | flops 2 | bytes 132705 | solution.py:109
  170.2 50.7 %custom-call.42 = f32[5,128,128]{1,2,0:T(8,128)} custom-call(f32[5,128,128]{2,1,0:T(8,128)} %get-tuple-element.10), custom_call_target="InvertDiagBlocksLowerTriangular" | custom-call | tf_op jit(solution)/shard_map/triangular_solve | solution.py:109
  234.0 4.7 collective-permute-start.11
  238.7 5.0 fusion.240
  245.6 4.4 collective-permute-start.13
  264.7 4.4 collective-permute-start.17
  269.2 6.9 collective-permute-done.16
  285.2 26.6 %collective-permute-done.18 = f32[3,512,256]{2,1,0:T(8,128)S(1)} collective-permute-done((f32[3,512,256]{2,1,0:T(8,128)S(1)}, f32[3,512,256]{2,1,0:T(8,128)S(1)}, u32[]{:S(2)}, u32[]{:S(2)}) %collective-permute-start.18) | collective-permute-done | bytes 1572896 | tf_op jit(solution)/shard_map/ppermute | solution.py:21
  324.1 32.9 %psum.64 = f32[256]{0:T(256)S(1)} all-reduce(f32[256]{0:T(256)S(1)} %get-tuple-element.11), channel_id=1, replica_groups=mesh['gx'=16,'gy'=2] {'gx'}, use_global_device_ids=true, to_apply=%region_13.15 | all-reduce | flops 256 | bytes 2048 | tf_op jit(solution)/shard_map/psum | solution.py:178
  357.1 5.4 psum.65
  362.4 36.9 %psum.63 = f32[256]{0:T(256)S(1)} all-reduce(f32[256]{0:T(256)S(1)} %get-tuple-element.12), channel_id=1, replica_groups=mesh['gx'=16,'gy'=2] {'gx','gy'}, use_global_device_ids=true, to_apply=%region_11.13 | all-reduce | flops 256 | bytes 2048 | tf_op jit(solution)/shard_map/psum | solution.py:61
  406.3 5.2 collective-permute-done.20
  411.5 4.7 collective-permute-done.21
  417.6 4.6 collective-permute-start.23
  426.5 4.4 collective-permute-start.25
  433.6 4.4 collective-permute-start.26
  439.9 4.7 collective-permute-done.26
  450.1 39.4 %psum.66 = f32[256]{0:T(256)S(1)} all-reduce(f32[256]{0:T(256)S(1)} %get-tuple-element.126), channel_id=1, replica_groups=mesh['gx'=16,'gy'=2] {'gx','gy'}, use_global_device_ids=true, to_apply=%region_16.18 | all-reduce | flops 256 | bytes 2048 | tf_op jit(solution)/shard_map/psum | solution.py:61
  490.7 4.4 collective-permute-start.29
  495.2 7.0 collective-permute-done.28
  502.3 4.3 collective-permute-start.30
  513.8 23.5 %collective-permute-done.30 = f32[3,512,256]{2,1,0:T(8,128)S(1)} collective-permute-done((f32[3,512,256]{2,1,0:T(8,128)S(1)}, f32[3,512,256]{2,1,0:T(8,128)S(1)}, u32[]{:S(2)}, u32[]{:S(2)}) %collective-permute-start.30) | collective-permute-done | bytes 1572896 | tf_op jit(solution)/shard_map/ppermute | solution.py:21
  549.7 35.1 %psum.67 = f32[256]{0:T(256)S(1)} all-reduce(f32[256]{0:T(256)S(1)} %get-tuple-element.128), channel_id=1, replica_groups=mesh['gx'=16,'gy'=2] {'gx'}, use_global_device_ids=true, to_apply=%region_18.20 | all-reduce | flops 256 | bytes 2048 | tf_op jit(solution)/shard_map/psum | solution.py:178
  584.7 5.4 psum.68
  594.5 4.7 collective-permute-done.32
  599.2 4.7 collective-permute-done.33
  605.3 4.6 collective-permute-start.35
  614.2 4.4 collective-permute-start.37
  621.3 4.4 collective-permute-start.38
  636.0 37.2 %psum.69 = f32[256]{0:T(256)S(1)} all-reduce(f32[256]{0:T(256)S(1)} %get-tuple-element.130), channel_id=1, replica_groups=mesh['gx'=16,'gy'=2] {'gx','gy'}, use_global_device_ids=true, to_apply=%region_21.23 | all-reduce | flops 256 | bytes 2048 | tf_op jit(solution)/shard_map/psum | solution.py:61
  673.4 4.4 collective-permute-start.41
  677.9 7.0 collective-permute-done.40
  684.9 4.3 collective-permute-start.42
  696.3 25.6 %collective-permute-done.42 = f32[3,512,256]{2,1,0:T(8,128)S(1)} collective-permute-done((f32[3,512,256]{2,1,0:T(8,128)S(1)}, f32[3,512,256]{2,1,0:T(8,128)S(1)}, u32[]{:S(2)}, u32[]{:S(2)}) %collective-permute-start.42) | collective-permute-done | bytes 1572896 | tf_op jit(solution)/shard_map/ppermute | solution.py:21
  733.5 34.7 %psum.70 = f32[256]{0:T(256)S(1)} all-reduce(f32[256]{0:T(256)S(1)} %get-tuple-element.132), channel_id=1, replica_groups=mesh['gx'=16,'gy'=2] {'gx'}, use_global_device_ids=true, to_apply=%region_23.25 | all-reduce | flops 256 | bytes 2048 | tf_op jit(solution)/shard_map/psum | solution.py:178
  768.2 5.4 psum.71
  (259 shorter events, 191.2 us)
Async XLA Ops:
  0.6 19.3 %copy-start = (f32[1,1,512,256]{3,2,1,0:T(8,128)S(1)}, f32[1,1,512,256]{3,2,1,0:T(8,128)}, u32[]{:S(2)}) copy-start(f32[1,1,512,256]{3,2,1,0:T(8,128)} %param.6) | copy-start | bytes 1572868
  0.7 13.4 %collective-permute-start.4 = (s32[128]{0:T(128)}, s32[128]{0:T(128)S(1)}, u32[]{:S(2)}, u32[]{:S(2)}) collective-permute-start(s32[128]{0:T(128)} %bitcast.373), channel_id=1, source_target_pairs={{0,2},{2,4},{4,6},{6,8},{8,10},{10,12},{12,14},{14,16},{16,18},{18... | collective-permute-start | bytes 1544 | tf_op jit(solution)/shard_map/ppermute | solution.py:15
  1.2 12.8 %collective-permute-start.5 = (s32[128]{0:T(128)}, s32[128]{0:T(128)S(1)}, u32[]{:S(2)}, u32[]{:S(2)}) collective-permute-start(s32[128]{0:T(128)} %bitcast.374), channel_id=1, source_target_pairs={{0,30},{2,0},{4,2},{6,4},{8,6},{10,8},{12,10},{14,12},{16,14},{18,... | collective-permute-start | bytes 1544 | tf_op jit(solution)/shard_map/ppermute | solution.py:15
  7.0 16.5 %collective-permute-start = (f32[3,512]{1,0:T(4,128)S(1)}, f32[3,512]{1,0:T(4,128)S(1)}, u32[]{:S(2)}, u32[]{:S(2)}) collective-permute-start(f32[3,512]{1,0:T(4,128)S(1)} %get-tuple-element.108), channel_id=1, source_target_pairs={{0,2},{2,4},{4,6},{6,8},{8,10},{10,12},{12,14},{14,16},{16,18},{18... | collective-permute-start | bytes 18440 | tf_op jit(solution)/shard_map/ppermute | solution.py:15
  7.0 16.4 %collective-permute-start.1 = (f32[3,512]{1,0:T(4,128)S(1)}, f32[3,512]{1,0:T(4,128)S(1)}, u32[]{:S(2)}, u32[]{:S(2)}) collective-permute-start(f32[3,512]{1,0:T(4,128)S(1)} %get-tuple-element.108), channel_id=1, source_target_pairs={{0,30},{2,0},{4,2},{6,4},{8,6},{10,8},{12,10},{14,12},{16,14},{18,... | collective-permute-start | bytes 18440 | tf_op jit(solution)/shard_map/ppermute | solution.py:15
  14.1 6.7 collective-permute-start.7
  15.4 6.3 collective-permute-start.6
  23.4 208.0 %collective-permute-start.8 = (f32[3,128,256]{2,1,0:T(8,128)}, f32[3,128,256]{2,1,0:T(8,128)}, u32[]{:S(2)}, u32[]{:S(2)}) collective-permute-start(f32[3,128,256]{2,1,0:T(8,128)} %pad_maximum_fusion.3), channel_id=1, source_target_pairs={{0,30},{2,0},{4,2},{6,4},{8,6},{10,8},{12,10},{14,12},{16,14},{18,... | collective-permute-start | bytes 1179656 | tf_op jit(solution)/shard_map/ppermute | solution.py:15
  23.5 7.5 collective-permute-start.2
  27.2 5.7 collective-permute-start.3
  29.3 202.2 %collective-permute-start.9 = (f32[3,128,256]{2,1,0:T(8,128)}, f32[3,128,256]{2,1,0:T(8,128)}, u32[]{:S(2)}, u32[]{:S(2)}) collective-permute-start(f32[3,128,256]{2,1,0:T(8,128)} %pad_maximum_fusion.4), channel_id=1, source_target_pairs={{0,2},{2,4},{4,6},{6,8},{8,10},{10,12},{12,14},{14,16},{16,18},{18... | collective-permute-start | bytes 1179656 | tf_op jit(solution)/shard_map/ppermute | solution.py:15
  170.2 54.7 %copy-start.3 = (f32[640,640]{1,0:T(8,128)S(1)}, f32[640,640]{1,0:T(8,128)}, u32[]{:S(2)}) copy-start(f32[640,640]{1,0:T(8,128)} %fusion.25) | copy-start | bytes 4915204
  232.7 11.1 %collective-permute-start.10 = (f32[128,256]{1,0:T(8,128)S(1)}, f32[128,256]{1,0:T(8,128)S(1)}, u32[]{:S(2)}, u32[]{:S(2)}) collective-permute-start(f32[128,256]{1,0:T(8,128)S(1)} %get-tuple-element.58), channel_id=1, source_target_pairs={{1,0},{3,2},{5,4},{7,6},{9,8},{11,10},{13,12},{15,14},{17,16},{19,... | collective-permute-start | bytes 393224 | tf_op jit(solution)/shard_map/ppermute | solution.py:21
  234.0 9.8 %collective-permute-start.11 = (f32[128,256]{1,0:T(8,128)S(1)}, f32[128,256]{1,0:T(8,128)S(1)}, u32[]{:S(2)}, u32[]{:S(2)}) collective-permute-start(f32[128,256]{1,0:T(8,128)S(1)} %get-tuple-element.59), channel_id=1, source_target_pairs={{0,1},{2,3},{4,5},{6,7},{8,9},{10,11},{12,13},{14,15},{16,17},{18,... | collective-permute-start | bytes 393224 | tf_op jit(solution)/shard_map/ppermute | solution.py:21
  245.6 7.1 collective-permute-start.12
  245.6 7.1 collective-permute-start.13
  252.7 6.9 collective-permute-start.14
  254.4 9.7 %collective-permute-start.15 = (f32[3,128,256]{2,1,0:T(8,128)S(1)}, f32[3,128,256]{2,1,0:T(8,128)S(1)}, u32[]{:S(2)}, u32[]{:S(2)}) collective-permute-start(f32[3,128,256]{2,1,0:T(8,128)S(1)} %pad_maximum_fusion.5), channel_id=1, source_target_pairs={{1,0},{3,2},{5,4},{7,6},{9,8},{11,10},{13,12},{15,14},{17,16},{19,... | collective-permute-start | bytes 1179656 | tf_op jit(solution)/shard_map/ppermute | solution.py:21
  264.7 11.5 %collective-permute-start.16 = (f32[512,256]{1,0:T(8,128)S(1)}, f32[512,256]{1,0:T(8,128)S(1)}, u32[]{:S(2)}, u32[]{:S(2)}) collective-permute-start(f32[512,256]{1,0:T(8,128)S(1)} %convolution_add_fusion.5), channel_id=1, source_target_pairs={{0,2},{2,4},{4,6},{6,8},{8,10},{10,12},{12,14},{14,16},{16,18},{18... | collective-permute-start | bytes 1572872 | tf_op jit(solution)/shard_map/ppermute | solution.py:15
  264.7 11.4 %collective-permute-start.17 = (f32[512,256]{1,0:T(8,128)S(1)}, f32[512,256]{1,0:T(8,128)S(1)}, u32[]{:S(2)}, u32[]{:S(2)}) collective-permute-start(f32[512,256]{1,0:T(8,128)S(1)} %convolution_add_fusion.5), channel_id=1, source_target_pairs={{0,30},{2,0},{4,2},{6,4},{8,6},{10,8},{12,10},{14,12},{16,14},{18,... | collective-permute-start | bytes 1572872 | tf_op jit(solution)/shard_map/ppermute | solution.py:15
  276.3 35.5 %collective-permute-start.18 = (f32[3,512,256]{2,1,0:T(8,128)S(1)}, f32[3,512,256]{2,1,0:T(8,128)S(1)}, u32[]{:S(2)}, u32[]{:S(2)}) collective-permute-start(f32[3,512,256]{2,1,0:T(8,128)S(1)} %pad_maximum_fusion), channel_id=1, source_target_pairs={{0,1},{2,3},{4,5},{6,7},{8,9},{10,11},{12,13},{14,15},{16,17},{18,... | collective-permute-start | bytes 4718600 | tf_op jit(solution)/shard_map/ppermute | solution.py:21
  277.9 39.5 %collective-permute-start.19 = (f32[3,512,256]{2,1,0:T(8,128)S(1)}, f32[3,512,256]{2,1,0:T(8,128)S(1)}, u32[]{:S(2)}, u32[]{:S(2)}) collective-permute-start(f32[3,512,256]{2,1,0:T(8,128)S(1)} %pad_maximum_fusion), channel_id=1, source_target_pairs={{1,0},{3,2},{5,4},{7,6},{9,8},{11,10},{13,12},{15,14},{17,16},{19,... | collective-permute-start | bytes 4718600 | tf_op jit(solution)/shard_map/ppermute | solution.py:21
  403.0 8.5 %collective-permute-start.20 = (f32[3,128,256]{2,1,0:T(8,128)S(1)}, f32[3,128,256]{2,1,0:T(8,128)S(1)}, u32[]{:S(2)}, u32[]{:S(2)}) collective-permute-start(f32[3,128,256]{2,1,0:T(8,128)S(1)} %pad_maximum_fusion.6), channel_id=1, source_target_pairs={{0,30},{2,0},{4,2},{6,4},{8,6},{10,8},{12,10},{14,12},{16,14},{18,... | collective-permute-start | bytes 1179656 | tf_op jit(solution)/shard_map/ppermute | solution.py:15
  406.2 10.0 %collective-permute-start.21 = (f32[3,128,256]{2,1,0:T(8,128)S(1)}, f32[3,128,256]{2,1,0:T(8,128)S(1)}, u32[]{:S(2)}, u32[]{:S(2)}) collective-permute-start(f32[3,128,256]{2,1,0:T(8,128)S(1)} %pad_maximum_fusion.7), channel_id=1, source_target_pairs={{0,2},{2,4},{4,6},{6,8},{8,10},{10,12},{12,14},{14,16},{16,18},{18... | collective-permute-start | bytes 1179656 | tf_op jit(solution)/shard_map/ppermute | solution.py:15
  416.3 6.9 collective-permute-start.22
  417.6 7.1 collective-permute-start.23
  426.4 7.1 collective-permute-start.24
  426.5 7.1 collective-permute-start.25
  433.6 11.0 %collective-permute-start.26 = (f32[3,128,256]{2,1,0:T(8,128)S(1)}, f32[3,128,256]{2,1,0:T(8,128)S(1)}, u32[]{:S(2)}, u32[]{:S(2)}) collective-permute-start(f32[3,128,256]{2,1,0:T(8,128)S(1)} %pad_maximum_fusion.8), channel_id=1, source_target_pairs={{0,1},{2,3},{4,5},{6,7},{8,9},{10,11},{12,13},{14,15},{16,17},{18,... | collective-permute-start | bytes 1179656 | tf_op jit(solution)/shard_map/ppermute | solution.py:21
  437.9 10.7 %collective-permute-start.27 = (f32[3,128,256]{2,1,0:T(8,128)S(1)}, f32[3,128,256]{2,1,0:T(8,128)S(1)}, u32[]{:S(2)}, u32[]{:S(2)}) collective-permute-start(f32[3,128,256]{2,1,0:T(8,128)S(1)} %pad_maximum_fusion.8), channel_id=1, source_target_pairs={{1,0},{3,2},{5,4},{7,6},{9,8},{11,10},{13,12},{15,14},{17,16},{19,... | collective-permute-start | bytes 1179656 | tf_op jit(solution)/shard_map/ppermute | solution.py:21
  490.7 56.2 %copy-start.1 = (f32[512,256]{1,0:T(8,128)}, f32[512,256]{1,0:T(8,128)S(1)}, u32[]{:S(2)}) copy-start(f32[512,256]{1,0:T(8,128)S(1)} %multiply_add_fusion.1) | copy-start | bytes 1572868
  490.7 11.5 %collective-permute-start.28 = (f32[512,256]{1,0:T(8,128)S(1)}, f32[512,256]{1,0:T(8,128)S(1)}, u32[]{:S(2)}, u32[]{:S(2)}) collective-permute-start(f32[512,256]{1,0:T(8,128)S(1)} %multiply_add_fusion.1), channel_id=1, source_target_pairs={{0,2},{2,4},{4,6},{6,8},{8,10},{10,12},{12,14},{14,16},{16,18},{18... | collective-permute-start | bytes 1572872 | tf_op jit(solution)/shard_map/ppermute | solution.py:15
  490.7 11.4 %collective-permute-start.29 = (f32[512,256]{1,0:T(8,128)S(1)}, f32[512,256]{1,0:T(8,128)S(1)}, u32[]{:S(2)}, u32[]{:S(2)}) collective-permute-start(f32[512,256]{1,0:T(8,128)S(1)} %multiply_add_fusion.1), channel_id=1, source_target_pairs={{0,30},{2,0},{4,2},{6,4},{8,6},{10,8},{12,10},{14,12},{16,14},{18,... | collective-permute-start | bytes 1572872 | tf_op jit(solution)/shard_map/ppermute | solution.py:15
  502.3 35.1 %collective-permute-start.30 = (f32[3,512,256]{2,1,0:T(8,128)S(1)}, f32[3,512,256]{2,1,0:T(8,128)S(1)}, u32[]{:S(2)}, u32[]{:S(2)}) collective-permute-start(f32[3,512,256]{2,1,0:T(8,128)S(1)} %pad_maximum_fusion.1), channel_id=1, source_target_pairs={{0,1},{2,3},{4,5},{6,7},{8,9},{10,11},{12,13},{14,15},{16,17},{18,... | collective-permute-start | bytes 4718600 | tf_op jit(solution)/shard_map/ppermute | solution.py:21
  506.5 36.4 %collective-permute-start.31 = (f32[3,512,256]{2,1,0:T(8,128)S(1)}, f32[3,512,256]{2,1,0:T(8,128)S(1)}, u32[]{:S(2)}, u32[]{:S(2)}) collective-permute-start(f32[3,512,256]{2,1,0:T(8,128)S(1)} %pad_maximum_fusion.1), channel_id=1, source_target_pairs={{1,0},{3,2},{5,4},{7,6},{9,8},{11,10},{13,12},{15,14},{17,16},{19,... | collective-permute-start | bytes 4718600 | tf_op jit(solution)/shard_map/ppermute | solution.py:21
  593.8 5.4 collective-permute-start.32
  593.9 10.0 %collective-permute-start.33 = (f32[3,128,256]{2,1,0:T(8,128)S(1)}, f32[3,128,256]{2,1,0:T(8,128)S(1)}, u32[]{:S(2)}, u32[]{:S(2)}) collective-permute-start(f32[3,128,256]{2,1,0:T(8,128)S(1)} %pad_maximum_fusion.10), channel_id=1, source_target_pairs={{0,2},{2,4},{4,6},{6,8},{8,10},{10,12},{12,14},{14,16},{16,18},{18... | collective-permute-start | bytes 1179656 | tf_op jit(solution)/shard_map/ppermute | solution.py:15
  604.0 6.9 collective-permute-start.34
  605.3 7.1 collective-permute-start.35
  614.1 7.1 collective-permute-start.36
  614.2 7.1 collective-permute-start.37
  621.3 9.6 %collective-permute-start.38 = (f32[3,128,256]{2,1,0:T(8,128)S(1)}, f32[3,128,256]{2,1,0:T(8,128)S(1)}, u32[]{:S(2)}, u32[]{:S(2)}) collective-permute-start(f32[3,128,256]{2,1,0:T(8,128)S(1)} %pad_maximum_fusion.11), channel_id=1, source_target_pairs={{0,1},{2,3},{4,5},{6,7},{8,9},{10,11},{12,13},{14,15},{16,17},{18,... | collective-permute-start | bytes 1179656 | tf_op jit(solution)/shard_map/ppermute | solution.py:21
  625.7 9.7 %collective-permute-start.39 = (f32[3,128,256]{2,1,0:T(8,128)S(1)}, f32[3,128,256]{2,1,0:T(8,128)S(1)}, u32[]{:S(2)}, u32[]{:S(2)}) collective-permute-start(f32[3,128,256]{2,1,0:T(8,128)S(1)} %pad_maximum_fusion.11), channel_id=1, source_target_pairs={{1,0},{3,2},{5,4},{7,6},{9,8},{11,10},{13,12},{15,14},{17,16},{19,... | collective-permute-start | bytes 1179656 | tf_op jit(solution)/shard_map/ppermute | solution.py:21
  631.5 41.8 %copy-start.2 = (f32[512,256]{1,0:T(8,128)S(1)}, f32[512,256]{1,0:T(8,128)}, u32[]{:S(2)}) copy-start(f32[512,256]{1,0:T(8,128)} %copy-done.1) | copy-start | bytes 1572868
  673.4 11.5 %collective-permute-start.40 = (f32[512,256]{1,0:T(8,128)S(1)}, f32[512,256]{1,0:T(8,128)S(1)}, u32[]{:S(2)}, u32[]{:S(2)}) collective-permute-start(f32[512,256]{1,0:T(8,128)S(1)} %multiply_add_fusion), channel_id=1, source_target_pairs={{0,2},{2,4},{4,6},{6,8},{8,10},{10,12},{12,14},{14,16},{16,18},{18... | collective-permute-start | bytes 1572872 | tf_op jit(solution)/shard_map/ppermute | solution.py:15
  673.4 11.4 %collective-permute-start.41 = (f32[512,256]{1,0:T(8,128)S(1)}, f32[512,256]{1,0:T(8,128)S(1)}, u32[]{:S(2)}, u32[]{:S(2)}) collective-permute-start(f32[512,256]{1,0:T(8,128)S(1)} %multiply_add_fusion), channel_id=1, source_target_pairs={{0,30},{2,0},{4,2},{6,4},{8,6},{10,8},{12,10},{14,12},{16,14},{18,... | collective-permute-start | bytes 1572872 | tf_op jit(solution)/shard_map/ppermute | solution.py:15
  684.9 37.0 %collective-permute-start.42 = (f32[3,512,256]{2,1,0:T(8,128)S(1)}, f32[3,512,256]{2,1,0:T(8,128)S(1)}, u32[]{:S(2)}, u32[]{:S(2)}) collective-permute-start(f32[3,512,256]{2,1,0:T(8,128)S(1)} %pad_maximum_fusion.2), channel_id=1, source_target_pairs={{0,1},{2,3},{4,5},{6,7},{8,9},{10,11},{12,13},{14,15},{16,17},{18,... | collective-permute-start | bytes 4718600 | tf_op jit(solution)/shard_map/ppermute | solution.py:21
  689.2 38.3 %collective-permute-start.43 = (f32[3,512,256]{2,1,0:T(8,128)S(1)}, f32[3,512,256]{2,1,0:T(8,128)S(1)}, u32[]{:S(2)}, u32[]{:S(2)}) collective-permute-start(f32[3,512,256]{2,1,0:T(8,128)S(1)} %pad_maximum_fusion.2), channel_id=1, source_target_pairs={{1,0},{3,2},{5,4},{7,6},{9,8},{11,10},{13,12},{15,14},{17,16},{19,... | collective-permute-start | bytes 4718600 | tf_op jit(solution)/shard_map/ppermute | solution.py:21
  (5 other events, 28.5 us)
